TPU v7x, 32 devices: a whole 2x2x4 slice. The times are simulated.
32 devices in a mesh: ctx: 8 (over z, y), heads: 4 (over x, core).
Axes of the slice: x: 2, y: 2, z: 4, core: 2. Of those that a mesh axis runs over, the one named last changes fastest.
Arguments:
- queries: bfloat16 [8192, 4096], P('ctx', 'heads'), may hold values from -8 to 8
- keys: bfloat16 [8192, 4096], P('ctx', 'heads'), may hold values from -8 to 8
- values: bfloat16 [8192, 4096], P('ctx', 'heads'), may hold values from -8 to 8
- gate_bias: float32 [32], P('heads'), may hold values from -2 to 2
- out_weight: bfloat16 [4096, 4096], P('heads'), may hold values from -0.09375 to 0.09375
Outputs:
- layer_out: bfloat16 [8192, 4096], P('ctx', 'heads')
All inputs are finite; a program needn't handle non-finite values.
Results may differ from a plain program's by a relative error of at most 0.0051.
Values may be sent and summed in bfloat16 or wider, within the bound.
A program may use at most 128 MiB of HBM per device.

v0:
```python
import math

import jax
import jax.numpy as jnp
from jax import lax
from jax.sharding import PartitionSpec as P

HD = 128


masked_score = -1e30


def features(inputs):
    return jax.nn.elu(inputs) + 1.0


def local_attention(query_heads, key_heads, value_heads):
    tok_rows = query_heads.shape[0]
    block_rows = min(512, tok_rows)
    score_scale = 1.0 / math.sqrt(HD)
    outputs = []
    for block_index in range(tok_rows // block_rows):
        first_query = block_index * block_rows
        key_end = first_query + block_rows
        scores = (
            jnp.einsum(
                "qhd,khd->hqk",
                query_heads[first_query:key_end],
                key_heads[:key_end],
                preferred_element_type=jnp.float32,
            )
            * score_scale
        )
        query_pos = first_query + lax.iota(jnp.int32, block_rows)
        key_pos = lax.iota(jnp.int32, key_end)
        allowed = key_pos[None, :] <= query_pos[:, None]
        scores = jnp.where(allowed[None], scores, masked_score)
        row_max = jnp.max(scores, axis=-1, keepdims=True)
        weights = jnp.exp(scores - row_max)
        probabilities = (weights / jnp.sum(weights, axis=-1, keepdims=True)).astype(jnp.bfloat16)
        outputs.append(
            jnp.einsum(
                "hqk,khd->qhd",
                probabilities,
                value_heads[:key_end],
                preferred_element_type=jnp.float32,
            )
        )
    return jnp.concatenate(outputs, axis=0)


def local(queries, keys, values, gate_bias, out_weight):
    tok_rows = queries.shape[0]
    local_heads = gate_bias.shape[0]
    highest = lax.Precision.HIGHEST
    query_heads = queries.reshape(tok_rows, local_heads, HD)
    key_heads = keys.reshape(tok_rows, local_heads, HD)
    value_heads = values.reshape(tok_rows, local_heads, HD)
    feat_key = features(key_heads.astype(jnp.float32))
    delta_memory = jnp.einsum(
        "thd,the->hde", feat_key, value_heads.astype(jnp.float32), precision=highest
    )
    delta_normal = jnp.sum(feat_key, axis=0)
    my_segment = lax.axis_index("ctx")
    gathered = (
        lax.all_gather(delta_memory[None], "ctx", axis=0, tiled=True),
        lax.all_gather(delta_normal[None], "ctx", axis=0, tiled=True),
    )
    row_count = gathered[0].shape[0]
    earlier = (lax.iota(jnp.int32, row_count) < my_segment).astype(jnp.float32)
    prior_memory = jnp.sum(earlier[:, None, None, None] * gathered[0], axis=0)
    prior_normal = jnp.sum(earlier[:, None, None] * gathered[1], axis=0)
    local_out = local_attention(query_heads, key_heads, value_heads)
    feat_query = features(query_heads.astype(jnp.float32))
    numer = jnp.einsum("thd,hde->the", feat_query, prior_memory, precision=highest)
    denom = jnp.maximum(jnp.einsum("thd,hd->th", feat_query, prior_normal, precision=highest), 1.0)
    retrieved = numer / denom[..., None]
    mix_gate = jax.nn.sigmoid(gate_bias)[None, :, None]
    attended = (mix_gate * retrieved + (1.0 - mix_gate) * local_out).astype(jnp.bfloat16)
    attended = attended.reshape(tok_rows, local_heads * HD)
    partial_terms = jnp.dot(attended, out_weight, preferred_element_type=jnp.float32)
    summed = lax.psum_scatter(partial_terms, "heads", scatter_dimension=1, tiled=True)
    return summed.astype(jnp.bfloat16)


def solution(mesh):
    return jax.shard_map(
        local,
        mesh=mesh,
        in_specs=(
            P("ctx", "heads"),
            P("ctx", "heads"),
            P("ctx", "heads"),
            P("heads"),
            P("heads", None),
        ),
        out_specs=P("ctx", "heads"),
        check_vma=False,
    )
```

profile of v0, /device:TPU:29, one launch (start us, length us, event | category | flops | bytes accessed | tf_op | source)
XLA Modules:
  0.0 273.3 jit_solution(10026259276073731455)
XLA Ops:
  6.5 8.0 %fusion.10 = f32[8,128,128]{2,1,0:T(8,128)} fusion(bf16[1024,1024]{1,0:T(8,128)(2,1)} %param.7, bf16[1024,1024]{1,0:T(8,128)(2,1)} %param.6), kind=kOutput, calls=%fused_computation.22 | convolution fusion | flops 1615855616 | bytes 4718592 | tf_op jit(solution)/shard_map/thd,the->hde/dot_general | solution.py:61
  14.6 1.5 copy-done
  16.1 1.9 fusion.16
  18.1 1.5 fusion.62
  19.5 1.6 copy.70
  21.1 2.3 copy.68
  23.5 1.3 copy.69
  24.8 1.3 copy.67
  26.1 25.1 %all_gather.7 = f32[8,8,128]{2,1,0:T(8,128)S(1)} all-gather(f32[1,8,128]{2,1,0:T(8,128)S(1)} %bitcast.81), channel_id=1, replica_groups=mesh['ctx'=8,'heads'=4] {'ctx'}, dimensions={0}, use_global_device_ids=true | all-gather | bytes 36864 | tf_op jit(solution)/shard_map/all_gather | solution.py:68
  51.1 0.1 multiply_reduce_fusion.1
  51.2 0.1 iota_compare_fusion.1
  51.3 6.5 %fusion.24 = f32[8,1,1024]{2,1,0:T(1,128)S(1)} fusion(f32[8,128,1]{1,2,0:T(1,128)S(1)} %bitcast.82, bf16[1024,1024]{1,0:T(8,128)(2,1)} %param.5), kind=kOutput, calls=%fused_computation.39 | convolution fusion | flops 17825792 | bytes 2134016 | tf_op jit(solution)/shard_map/thd,hd->th/dot_general | solution.py:77
  57.9 1.2 iota_compare_fusion
  59.0 8.1 %fusion.64 = (f32[8,512]{1,0:T(8,128)S(1)}, f32[8,512,512]{1,2,0:T(8,128)}) fusion(pred[512,512]{0,1:T(8,128)(4,1)S(1)} %iota_compare_fusion.1, bf16[512,8,128]{0,2,1:T(8,128)(2,1)} %bitcast.79, bf16[512,8,128]{0,2,1:T(8,128)(2,1)} %bitcast.80), kind=kOutput, calls=%fused_computation.80 | convolution fusion | flops 545260032 | bytes 10764288 | tf_op jit(solution)/shard_map/sub | solution.py:40
  67.1 8.5 %fusion.30 = f32[8,512,1024]{2,1,0:T(8,128)} fusion(bf16[512,8,128]{0,2,1:T(8,128)(2,1)S(1)} %bitcast.76, bf16[1024,1024]{1,0:T(8,128)(2,1)S(1)} %copy-done.1), kind=kOutput, calls=%fused_computation.43 | convolution fusion | flops 1073741824 | bytes 19922944 | tf_op jit(solution)/shard_map/qhd,khd->hqk/dot_general | solution.py:27
  75.6 2.0 fusion.43
  77.7 21.5 %fusion.63 = (f32[8,512]{1,0:T(8,128)S(1)}, f32[8,512,1024]{2,1,0:T(8,128)}) fusion(f32[8,512,1024]{2,1,0:T(8,128)} %fusion.30, pred[512,1024]{1,0:T(8,128)(4,1)S(1)} %copy-done.6), kind=kOutput, calls=%fused_computation.79 | output fusion | flops 25166848 | bytes 34095104 | tf_op jit(solution)/shard_map/sub | solution.py:40
  99.2 8.4 %fusion.44 = f32[512,8,128]{0,2,1:T(8,128)} fusion(f32[8,512,1024]{2,1,0:T(8,128)} %get-tuple-element.10, f32[8,512]{1,0:T(8,128)S(1)} %get-tuple-element.9, bf16[1024,1024]{1,0:T(8,128)(2,1)S(1)} %copy-done.2), kind=kOutput, calls=%fused_computation.58 | convolution fusion | flops 1082130432 | bytes 20987904 | tf_op jit(solution)/shard_map/hqk,khd->qhd/dot_general | solution.py:43
  107.6 2.9 %multiply_reduce_fusion = f32[8,128,128]{2,1,0:T(8,128)S(1)} fusion(f32[8,8,128,128]{3,2,1,0:T(8,128)} %bitcast.77, f32[8]{0:T(128)S(1)} %compare_convert_fusion), kind=kLoop, calls=%fused_computation.36 | loop fusion | flops 1966080 | bytes 4718624 | tf_op jit(solution)/shard_map/reduce_sum | solution.py:72
  110.5 0.5 copy-done.9
  111.1 7.6 %fusion.18 = bf16[1024,8,128]{0,2,1:T(8,128)(2,1)S(1)} fusion(f32[512,8,128]{0,2,1:T(8,128)} %fusion.44, f32[512,8,128]{0,2,1:T(8,128)S(1)} %copy-done.9, f32[8]{0:T(128)S(1)} %get-tuple-element.5, f32[1024,8]{0,1:T(8,128)S(1)} %fusion.51, f32[8]{0:T(128)S(1)} %get-tuple-element.6, f32[8,128,128]{2,1,0:T(8,128)S(1)} %multiply_reduce_fusion, ...), kind=kOutput, calls=%fused_computation.30 | convolution fusion | flops 1622147072 | bytes 8945728 | tf_op jit(solution)/shard_map/thd,hde->the/dot_general | solution.py:76
  118.7 11.5 %fusion.65 = f32[1024,4096]{1,0:T(8,128)} fusion(bf16[1024,1024]{0,1:T(8,128)(2,1)S(1)} %bitcast.85, bf16[1024,4096]{1,0:T(8,128)(2,1)S(1)} %bitcast.84), kind=kOutput, calls=%fused_computation.81 | convolution fusion | flops 8589934592 | bytes 27262976 | tf_op jit(solution)/shard_map/dot_general | solution.py:82
  130.3 132.3 %reduce-scatter.2.cloned.1.call-done = f32[1024,1024]{1,0:T(8,128)} async-done(((f32[1024,4096]{1,0:T(8,128)}), f32[1024,1024]{1,0:T(8,128)}) %reduce-scatter.2.cloned.1.call-update) | async-done | bytes 4194320 | tf_op jit(solution)/shard_map/reduce_scatter | solution.py:83
  262.6 3.8 %convert_element_type.44 = bf16[1024,1024]{1,0:T(8,128)(2,1)} convert(f32[1024,1024]{1,0:T(8,128)} %reduce-scatter.2.cloned.1.call-done) | non-fusion elementwise | flops 1048576 | bytes 6291456 | tf_op jit(solution)/shard_map/convert_element_type | solution.py:84
  (36 shorter events, 0.2 us)
Async XLA Ops:
  6.5 101.1 %all-gather.3.cloned.1.call-start = ((), (), s32[]{:S(2)}) async-start(), calls=%async_computation.2 | async-start | bytes 4718592 | tf_op jit(solution)/shard_map/all_gather | solution.py:67
  14.5 1.6 copy-start
  14.6 248.0 %reduce-scatter.2.cloned.1.call-start = ((), (), s32[]{:S(2)}) async-start(), calls=%async_computation.1 | async-start | bytes 20971520 | tf_op jit(solution)/shard_map/reduce_scatter | solution.py:83
  14.6 3.4 %copy-start.3 = (bf16[1024,1024]{1,0:T(8,128)(2,1)S(1)}, bf16[1024,1024]{1,0:T(8,128)(2,1)}, u32[]{:S(2)}) copy-start(bf16[1024,1024]{1,0:T(8,128)(2,1)} %param.5) | copy-start | bytes 6291460
  18.0 5.4 %slice-start = ((bf16[1024,1024]{1,0:T(8,128)(2,1)}), bf16[512,1024]{1,0:T(8,128)(2,1)S(1)}, s32[]{:S(2)}) async-start(bf16[1024,1024]{1,0:T(8,128)(2,1)} %param.6), calls=%async_computation.3 | async-start | bytes 2097152 | tf_op jit(solution)/shard_map/slice | solution.py:30
  19.5 5.2 %slice-start.1 = ((bf16[1024,1024]{1,0:T(8,128)(2,1)}), bf16[512,1024]{1,0:T(8,128)(2,1)S(1)}, s32[]{:S(2)}) async-start(bf16[1024,1024]{1,0:T(8,128)(2,1)} %param.7), calls=%async_computation.4 | async-start | bytes 2097152 | tf_op jit(solution)/shard_map/slice | solution.py:46
  19.5 31.8 %copy-start.7 = (f32[8]{0:T(128)S(1)}, f32[8]{0:T(128)}, u32[]{:S(2)}) copy-start(f32[8]{0:T(128)} %param.8) | copy-start | bytes 100
  59.0 8.1 %copy-start.1 = (bf16[1024,1024]{1,0:T(8,128)(2,1)S(1)}, bf16[1024,1024]{1,0:T(8,128)(2,1)}, u32[]{:S(2)}) copy-start(bf16[1024,1024]{1,0:T(8,128)(2,1)} %param.6) | copy-start | bytes 6291460
  67.1 8.5 %copy-start.5 = (bf16[512,1024]{0,1:T(8,128)(2,1)S(1)}, bf16[512,1024]{0,1:T(8,128)(2,1)}, u32[]{:S(2)}) copy-start(bf16[512,1024]{0,1:T(8,128)(2,1)} %copy.67) | copy-start | bytes 3145732
  67.1 8.5 %copy-start.8 = (f32[8,512,512]{1,2,0:T(8,128)S(1)}, f32[8,512,512]{1,2,0:T(8,128)}, u32[]{:S(2)}) copy-start(f32[8,512,512]{1,2,0:T(8,128)} %get-tuple-element.12) | copy-start | bytes 25165828
  75.6 2.1 copy-start.6
  77.7 21.5 %copy-start.2 = (bf16[1024,1024]{1,0:T(8,128)(2,1)S(1)}, bf16[1024,1024]{1,0:T(8,128)(2,1)}, u32[]{:S(2)}) copy-start(bf16[1024,1024]{1,0:T(8,128)(2,1)} %param.7) | copy-start | bytes 6291460
  107.6 2.9 %copy-start.4 = (bf16[1024,1024]{1,0:T(8,128)(2,1)S(1)}, bf16[1024,1024]{1,0:T(8,128)(2,1)}, u32[]{:S(2)}) copy-start(bf16[1024,1024]{1,0:T(8,128)(2,1)} %param.5) | copy-start | bytes 6291460
  107.6 3.5 %copy-start.9 = (f32[512,8,128]{0,2,1:T(8,128)S(1)}, f32[512,8,128]{0,2,1:T(8,128)}, u32[]{:S(2)}) copy-start(f32[512,8,128]{0,2,1:T(8,128)} %fusion.43) | copy-start | bytes 6291460
  107.6 11.1 %slice-start.2 = ((s8[8388608]{0:T(1024)(128)(4,1)}), s8[4194304]{0:T(1024)(128)(4,1)S(1)}, s32[]{:S(2)}) async-start(s8[8388608]{0:T(1024)(128)(4,1)} %bitcast.83), calls=%async_computation.5 | async-start | bytes 8388608
  111.1 7.7 %slice-start.3 = ((s8[8388608]{0:T(1024)(128)(4,1)}), s8[4194304]{0:T(1024)(128)(4,1)S(1)}, s32[]{:S(2)}) async-start(s8[8388608]{0:T(1024)(128)(4,1)} %bitcast.83), calls=%async_computation.6 | async-start | bytes 8388608
Sparse Core Ops, SparseCore 0:
  14.7 71.5 all-gather.2
  130.4 132.1 reduce-scatter.1
where the time goes:
time: 275 us; the launch traced here: 273 us
  waiting for transfers between devices  132 us (48%)
  matrix products  60.7 us (22%)
  other arithmetic  31.5 us (11%)
  blocking collectives  25.1 us (9%)
  between operations  13.5 us (5%)
  local copies, waits for them, and re-layouts  10.1 us (4%)
    reduce_scatter x1, waiting for transfers between devices, local(): lax.psum_scatter(partial_terms, 'heads', scatter_dimension=1, tiled=True)  132 us
    all_gather x1, blocking collectives, local(): lax.all_gather(delta_normal[None], 'ctx', axis=0, tiled=True)  25.1 us
    sub x1, other arithmetic, local_attention(): weights = jnp.exp(scores - row_max)  21.5 us
    dot_general x1, matrix products, local(): jnp.dot(attended, out_weight, preferred_element_type=jnp.float32)  11.5 us
    dot_general x2, matrix products, local_attention(): jnp.einsum('hqk,khd->qhd', probabilities, value_heads[:key_end], preferre...  10.4 us
    unnamed x28, local copies, waits for them, and re-layouts  8.6 us
    dot_general x1, matrix products, local_attention(): jnp.einsum('qhd,khd->hqk', query_heads[first_query:key_end], key_heads[:k...  8.52 us
    sub x1, matrix products, local_attention(): weights = jnp.exp(scores - row_max)  8.08 us
  transfers between devices with their start and end apart: 2, of which 1 were waited for; matrix products, arithmetic and copies ran while one was open for 24% of the time, Pallas kernels for 0%

commit v1 on v0

v1 whole, which is shorter than its diff:
```python
import functools
import math

import jax
import jax.numpy as jnp
from jax import lax
from jax.experimental import pallas as pl
from jax.experimental.pallas import tpu as pltpu
from jax.sharding import PartitionSpec as P

HD = 128
MEM_ROWS = HD + 16
MESH = pl.DeviceIdType.MESH
masked_score = -1e30
F32 = jnp.float32
BF16 = jnp.bfloat16


def features(x):
    return jnp.where(x > 0.0, x + 1.0, jnp.exp(jnp.minimum(x, 0.0)))


def nt_dot(a, b):
    return lax.dot_general(a, b, (((1,), (1,)), ((), ())), preferred_element_type=F32)


def tn_dot(a, b):
    return lax.dot_general(a, b, (((0,), (0,)), ((), ())), preferred_element_type=F32)


def kernel(
    n_ctx, n_heads, block, tile,
    q_hbm, k_hbm, v_hbm, w_hbm, gate_ref, out_hbm,
    q_ref, k_ref, v_ref, w_ref, gates, delta, partner_delta, pair_sum, slots, prior_sum, prior,
    mixed, own_rows, partner_rows, cross_out, cross_in, out_stage,
    in_sem, w_sem, w_send, w_recv, pd_send, pd_recv, ps_send, ps_recv,
    rows_send, rows_recv, cross_send, cross_recv, out_sem,
):
    seg = lax.axis_index("ctx")
    col = lax.axis_index("heads")
    core = col % 2
    chip = col // 2
    other_col = col + 1 - 2 * core
    odd = seg % 2
    pair = seg // 2
    other_seg = seg + 1 - 2 * odd
    n_pairs = n_ctx // 2
    n_chips = n_heads // 2
    tokens, width = q_ref.shape
    heads = width // HD
    n_blocks = tokens // block

    loads = [
        pltpu.make_async_copy(src, dst, in_sem.at[i])
        for i, (src, dst) in enumerate(((k_hbm, k_ref), (v_hbm, v_ref), (q_hbm, q_ref)))
    ]
    for load in loads:
        load.start()

    def w_cols(target_chip, target_core):
        first = pl.multiple_of((target_chip * 2 + target_core) * width, width)
        return w_hbm.at[:, pl.ds(first, width)]

    w_loads = [
        pltpu.make_async_copy(w_cols(t, core), w_ref.at[0, t], w_sem.at[t]) for t in range(n_chips)
    ]
    for load in w_loads:
        load.start()

    barrier = pltpu.get_barrier_semaphore()
    peers = [(seg, other_col), (other_seg, col)]
    for o in range(1, n_chips):
        peers.append((seg, lax.rem(chip + o, n_chips) * 2 + core))
    for o in range(1, n_pairs):
        peers.append((lax.rem(pair + o, n_pairs) * 2 + odd, col))
    for peer in peers:
        pl.semaphore_signal(barrier, inc=1, device_id=peer, device_id_type=MESH)
    pl.semaphore_wait(barrier, len(peers))

    def remote(src, dst, send, recv, peer):
        return pltpu.make_async_remote_copy(
            src_ref=src, dst_ref=dst, send_sem=send, recv_sem=recv,
            device_id=peer, device_id_type=MESH,
        )

    def w_copy(t):
        return remote(
            w_cols(t, 1 - core), w_ref.at[1, t], w_send.at[t], w_recv.at[t], (seg, other_col)
        )

    def delta_copy(h):
        return remote(
            delta.at[h], partner_delta.at[h], pd_send.at[h], pd_recv.at[h], (other_seg, col)
        )

    def pair_copy(o, h):
        peer = (lax.rem(pair + o, n_pairs) * 2 + odd, col)
        return remote(
            pair_sum.at[h], slots.at[o - 1, h], ps_send.at[o - 1, h], ps_recv.at[o - 1, h], peer
        )

    def rows_copy(b):
        rows = pl.ds(b * block, block)
        return remote(
            own_rows.at[rows], partner_rows.at[rows], rows_send.at[b], rows_recv.at[b],
            (seg, other_col),
        )

    def cross_copy(o, b):
        rows = pl.ds(b * block, block)
        peer = (seg, lax.rem(chip + o, n_chips) * 2 + core)
        return remote(
            cross_out.at[o - 1, rows], cross_in.at[o - 1, rows],
            cross_send.at[o - 1, b], cross_recv.at[o - 1, b], peer,
        )

    def head_cols(h):
        return pl.ds(pl.multiple_of(h * HD, HD), HD)

    for t in range(n_chips):
        w_copy(t).start()

    gate_values = 1.0 / (1.0 + jnp.exp(-gate_ref[...]))
    for h in range(heads):
        gates[0:1, h * HD : (h + 1) * HD] = jnp.broadcast_to(gate_values[0:1, h : h + 1], (1, HD))

    loads[0].wait()
    loads[1].wait()

    @pl.loop(0, heads)
    def _(h):
        feat = features(k_ref[:, head_cols(h)].astype(F32))
        memory = tn_dot(v_ref[:, head_cols(h)], feat.astype(BF16))
        normal = jnp.sum(feat, axis=0, keepdims=True)
        delta[h, 0:HD, :] = memory.astype(BF16)
        delta[h, HD:MEM_ROWS, :] = jnp.broadcast_to(normal, (MEM_ROWS - HD, HD)).astype(BF16)
        delta_copy(h).start()

    loads[2].wait()

    scale = math.log2(math.e) / math.sqrt(HD)

    def attend(h):
        cols = head_cols(h)
        gate = 1.0 - gates[0:1, cols]
        ones = jnp.ones((tokens, HD), BF16)
        value_ext = jnp.concatenate([v_ref[:, cols], ones], axis=1)
        keys = k_ref[:, cols]
        row_ids = lax.broadcasted_iota(jnp.int32, (block, block), 0)
        col_ids = lax.broadcasted_iota(jnp.int32, (block, block), 1)
        allowed = col_ids <= row_ids
        for b in range(n_blocks):
            first = b * block
            query = q_ref[first : first + block, cols]
            diag = nt_dot(query, keys[first : first + block])
            diag = jnp.where(allowed, diag * scale, masked_score)
            top = jnp.max(diag, axis=1, keepdims=True)
            if b:
                past = nt_dot(query, keys[:first]) * scale
                top = jnp.maximum(top, jnp.max(past, axis=1, keepdims=True))
            total = jnp.dot(
                jnp.exp2(diag - top).astype(BF16), value_ext[first : first + block],
                preferred_element_type=F32,
            )
            if b:
                total = total + jnp.dot(
                    jnp.exp2(past - top).astype(BF16), value_ext[:first],
                    preferred_element_type=F32,
                )
            mixed[first : first + block, cols] = gate * (total[:, :HD] / total[:, HD:])

    group = 2 if heads % 2 == 0 else 1
    rounds = heads // group
    chunk = min(2 * group, heads)
    chunks = pl.cdiv(heads, chunk)

    @pl.loop(0, rounds)
    def _(i):
        for g in range(group):
            attend(i * group + g)

        @pl.when(i < chunks)
        def _():
            @pl.loop(0, chunk)
            def _(c):
                h = i * chunk + c
                delta_copy(h).wait_recv()
                pair_sum[h] = (delta[h].astype(F32) + partner_delta[h].astype(F32)).astype(BF16)
                for o in range(1, n_pairs):
                    @pl.when(pair + o < n_pairs)
                    def _():
                        pair_copy(o, h).start()

    odd_mask = jnp.where(odd == 1, 1.0, 0.0).astype(F32)

    @pl.loop(0, heads)
    def _(h):
        prior_sum[h] = partner_delta[h].astype(F32) * odd_mask

    for o in range(1, n_pairs):
        @pl.when(pair >= o)
        def _():
            @pl.loop(0, heads)
            def _(h):
                pair_copy(o, h).wait_recv()
                prior_sum[h] += slots[o - 1, h].astype(F32)

    @pl.loop(0, heads)
    def _(h):
        prior[h, 0:HD, :] = prior_sum[h, 0:HD, :].astype(BF16)
        prior[h, HD : 2 * HD, :] = jnp.broadcast_to(
            prior_sum[h, HD : HD + 1, :], (HD, HD)
        ).astype(BF16)

    for t in range(n_chips):
        w_loads[t].wait()
        w_copy(t).wait_recv()

    def finish(b):
        rows = pl.ds(b * block, block)

        @pl.loop(0, heads // group)
        def _(i):
            for g in range(group):
                cols = head_cols(i * group + g)
                feat = features(q_ref[rows, cols].astype(F32)).astype(BF16)
                both = nt_dot(feat, prior[i * group + g])
                retrieved = both[:, :HD] / jnp.maximum(both[:, HD:], 1.0)
                own_rows[rows, cols] = (gates[0:1, cols] * retrieved + mixed[rows, cols]).astype(BF16)

        rows_copy(b).start()

    def product(b, target, t):
        rows = pl.ds(b * block, block)
        cols = pl.ds(pl.multiple_of(t * tile, tile), tile)
        return jnp.dot(
            own_rows[rows], w_ref[0, target, :, cols], preferred_element_type=F32
        ) + jnp.dot(
            partner_rows[rows], w_ref[1, target, :, cols], preferred_element_type=F32
        )

    def cross(b):
        rows_copy(b).wait_recv()
        for o in range(1, n_chips):
            target = lax.rem(chip + o, n_chips)

            @pl.loop(0, width // tile)
            def _(t):
                cols = pl.ds(pl.multiple_of(t * tile, tile), tile)
                cross_out[o - 1, pl.ds(b * block, block), cols] = product(b, target, t).astype(BF16)

            cross_copy(o, b).start()

    finish(0)
    for b in range(n_blocks):
        if b + 1 < n_blocks:
            finish(b + 1)
        cross(b)

    @pl.loop(0, n_blocks)
    def _(b):
        @pl.loop(0, width // tile)
        def _(t):
            cols = pl.ds(pl.multiple_of(t * tile, tile), tile)
            mixed[pl.ds(b * block, block), cols] = product(b, chip, t)

    def out_copy(b):
        rows = pl.ds(b * block, block)
        return pltpu.make_async_copy(out_stage.at[rows], out_hbm.at[rows], out_sem.at[b])

    for b in range(n_blocks):
        rows = pl.ds(b * block, block)
        total = mixed[rows]
        for o in range(1, n_chips):
            cross_copy(o, b).wait_recv()
            total = total + cross_in[o - 1, rows].astype(F32)
        out_stage[rows] = total.astype(BF16)
        out_copy(b).start()

    for t in range(n_chips):
        w_copy(t).wait_send()

    @pl.loop(0, heads)
    def _(h):
        delta_copy(h).wait_send()
        for o in range(1, n_pairs):
            @pl.when(pair + o < n_pairs)
            def _():
                pair_copy(o, h).wait_send()

    for b in range(n_blocks):
        rows_copy(b).wait_send()
        for o in range(1, n_chips):
            cross_copy(o, b).wait_send()
        out_copy(b).wait()


def local(n_ctx, n_heads, queries, keys, values, gate_bias, out_weight):
    tokens, width = queries.shape
    heads = gate_bias.shape[0]
    block = min(256, tokens)
    tile = min(512, width)
    n_blocks = tokens // block
    n_pairs = n_ctx // 2
    n_chips = n_heads // 2
    dma = pltpu.SemaphoreType.DMA
    far_pairs = max(n_pairs - 1, 1)
    far_chips = max(n_chips - 1, 1)
    hbm = pl.BlockSpec(memory_space=pl.ANY)
    memories = (heads, MEM_ROWS, HD)
    return pl.pallas_call(
        functools.partial(kernel, n_ctx, n_heads, block, tile),
        out_shape=jax.ShapeDtypeStruct((tokens, width), BF16),
        in_specs=[hbm, hbm, hbm, hbm, pl.BlockSpec(memory_space=pltpu.VMEM)],
        out_specs=hbm,
        scratch_shapes=[
            pltpu.VMEM((tokens, width), BF16),
            pltpu.VMEM((tokens, width), BF16),
            pltpu.VMEM((tokens, width), BF16),
            pltpu.VMEM((2, n_chips, width, width), BF16),
            pltpu.VMEM((1, width), F32),
            pltpu.VMEM(memories, BF16),
            pltpu.VMEM(memories, BF16),
            pltpu.VMEM(memories, BF16),
            pltpu.VMEM((far_pairs,) + memories, BF16),
            pltpu.VMEM(memories, F32),
            pltpu.VMEM((heads, 2 * HD, HD), BF16),
            pltpu.VMEM((tokens, width), F32),
            pltpu.VMEM((tokens, width), BF16),
            pltpu.VMEM((tokens, width), BF16),
            pltpu.VMEM((far_chips, tokens, width), BF16),
            pltpu.VMEM((far_chips, tokens, width), BF16),
            pltpu.VMEM((tokens, width), BF16),
            dma((3,)),
            dma((n_chips,)),
            dma((n_chips,)),
            dma((n_chips,)),
            dma((heads,)),
            dma((heads,)),
            dma((far_pairs, heads)),
            dma((far_pairs, heads)),
            dma((n_blocks,)),
            dma((n_blocks,)),
            dma((far_chips, n_blocks)),
            dma((far_chips, n_blocks)),
            dma((n_blocks,)),
        ],
        compiler_params=pltpu.CompilerParams(
            collective_id=0, has_side_effects=True, vmem_limit_bytes=60 * 1024 * 1024
        ),
    )(queries, keys, values, out_weight, gate_bias.reshape(1, heads))


def solution(mesh):
    return jax.shard_map(
        functools.partial(local, mesh.shape["ctx"], mesh.shape["heads"]),
        mesh=mesh,
        in_specs=(
            P("ctx", "heads"),
            P("ctx", "heads"),
            P("ctx", "heads"),
            P("heads"),
            P("heads", None),
        ),
        out_specs=P("ctx", "heads"),
        check_vma=False,
    )
```

time: 275 us -> 92.1 us (0.33)
  waiting for transfers between devices: 132 us -> 0 us
  Pallas kernels: 0 us -> 88.8 us
  matrix products: 60.7 us -> 0 us
  other arithmetic: 31.5 us -> 0 us
  blocking collectives: 25.1 us -> 0 us
  between operations: 13.5 us -> 0.01 us
  local copies, waits for them, and re-layouts: 10.1 us -> 3.08 us
    reduce_scatter x1 -> x0, waiting for transfers between devices: 132 us -> none  [local(): lax.psum_scatter(partial_terms, 'heads', scatter_dimension=1, tiled=True)]
    pallas_call x0 -> x1, Pallas kernels: none -> 88.8 us  [local(): pl.pallas_call(functools.partial(kernel, n_ctx, n_heads, block, tile), ou...]
    dot_general x7 -> x0, matrix products: 52.6 us -> none  [the longest x1 11.5 us: local(): jnp.dot(attended, out_weight, preferred_element_type=jnp.float32)]
    all_gather x1 -> x0, blocking collectives: 25.1 us -> none  [local(): lax.all_gather(delta_normal[None], 'ctx', axis=0, tiled=True)]
    sub x2 -> x0, other arithmetic: 21.5 us -> none  [the longest x1 21.5 us: local_attention(): weights = jnp.exp(scores - row_max)]
    sub x1 -> x0, matrix products: 8.08 us -> none  [local_attention(): weights = jnp.exp(scores - row_max)]
    unnamed x28 -> x1, local copies, waits for them, and re-layouts: 8.6 us -> 3.08 us
    reduce_sum x3 -> x0, other arithmetic: 4.89 us -> none  [the longest x1 2.91 us: local(): prior_memory = jnp.sum(earlier[:, None, None, None] * gathered[0], axis=0)]
  transfers between devices with their start and end apart: 2 -> 0, of which waited for: 1 -> 0; matrix products, arithmetic and copies ran while one was open for 24% -> 0% of each run, Pallas kernels for 0% -> 0%
where the time goes in v1:
time: 92.1 us; the launch traced here: 91.9 us
  Pallas kernels  88.8 us (96%)
  local copies, waits for them, and re-layouts  3.08 us (3%)
    pallas_call x1, Pallas kernels, local(): pl.pallas_call(functools.partial(kernel, n_ctx, n_heads, block, tile), ou...  88.8 us
    unnamed x1, local copies, waits for them, and re-layouts  3.08 us

profile of v1, /device:TPU:29, one launch (start us, length us, event | category | flops | bytes accessed | tf_op | source)
XLA Modules:
  0.0 91.9 jit_solution(4684005300156142707)
XLA Ops:
  0.0 88.8 %shard_map.55 = bf16[1024,1024]{1,0:T(8,128)(2,1)} custom-call(bf16[1024,1024]{1,0:T(8,128)(2,1)} %q_hbm.1, bf16[1024,1024]{1,0:T(8,128)(2,1)} %k_hbm.1, bf16[1024,1024]{1,0:T(8,128)(2,1)} %v_hbm.1, bf16[1024,4096]{1,0:T(8,128)(2,1)} %w_hbm.1, f32[1,8]{1,0:T(1,128)} %bitcast.1), custom_call_target="tpu_custom_call" | custom-call | tf_op jit(solution)/shard_map/pallas_call | solution.py:311
  88.8 3.1 %copy.7 = bf16[1024,1024]{1,0:T(8,128)(2,1)} copy(bf16[1024,1024]{1,0:T(8,128)(2,1)} %shard_map.55) | data formatting | bytes 4194304

commit v2 on v1

v2 whole, which is shorter than its diff:
```python
import functools
import math

import jax
import jax.numpy as jnp
from jax import lax
from jax.experimental import pallas as pl
from jax.experimental.pallas import tpu as pltpu
from jax.sharding import PartitionSpec as P

HD = 128
MEM_ROWS = HD + 16
MESH = pl.DeviceIdType.MESH
masked_score = -1e30
F32 = jnp.float32
BF16 = jnp.bfloat16


def features(x):
    return jnp.where(x > 0.0, x + 1.0, jnp.exp(jnp.minimum(x, 0.0)))


def nt_dot(a, b):
    return lax.dot_general(a, b, (((1,), (1,)), ((), ())), preferred_element_type=F32)


def tn_dot(a, b):
    return lax.dot_general(a, b, (((0,), (0,)), ((), ())), preferred_element_type=F32)


def kernel(
    n_ctx, n_heads, block, blocks, tile,
    q_hbm, k_hbm, v_hbm, w_hbm, gate_ref, out_ref,
    q_ref, k_ref, v_ref, w_ref, gates, delta, partner_delta, running, arrived, prior,
    mixed, own_rows, partner_rows, cross_out, cross_in,
    in_sem, w_sem, w_send, w_recv, pd_send, pd_recv, run_send, run_recv,
    rows_send, rows_recv, cross_send, cross_recv,
):
    seg = lax.axis_index("ctx")
    col = lax.axis_index("heads")
    core = col % 2
    chip = col // 2
    other_col = col + 1 - 2 * core
    odd = seg % 2
    pair = seg // 2
    other_seg = seg + 1 - 2 * odd
    n_pairs = n_ctx // 2
    n_chips = n_heads // 2
    tokens, width = q_ref.shape
    heads = width // HD
    n_blocks = len(blocks)

    loads = [
        pltpu.make_async_copy(src, dst, in_sem.at[i])
        for i, (src, dst) in enumerate(((k_hbm, k_ref), (v_hbm, v_ref), (q_hbm, q_ref)))
    ]
    loads[0].start()
    loads[1].start()

    def w_cols(target_chip, target_core):
        first = pl.multiple_of((target_chip * 2 + target_core) * width, width)
        return w_hbm.at[:, pl.ds(first, width)]

    w_loads = [
        pltpu.make_async_copy(w_cols(t, core), w_ref.at[0, t], w_sem.at[t]) for t in range(n_chips)
    ]

    barrier = pltpu.get_barrier_semaphore()
    peers = [(seg, other_col), (other_seg, col)]
    for o in range(1, n_chips):
        peers.append((seg, lax.rem(chip + o, n_chips) * 2 + core))
    for o in (1, n_pairs - 1):
        peers.append((lax.rem(pair + o, n_pairs) * 2 + odd, col))
    for peer in peers:
        pl.semaphore_signal(barrier, inc=1, device_id=peer, device_id_type=MESH)
    pl.semaphore_wait(barrier, len(peers))

    def remote(src, dst, send, recv, peer):
        return pltpu.make_async_remote_copy(
            src_ref=src, dst_ref=dst, send_sem=send, recv_sem=recv,
            device_id=peer, device_id_type=MESH,
        )

    def w_copy(t):
        return remote(
            w_cols(t, 1 - core), w_ref.at[1, t], w_send.at[t], w_recv.at[t], (seg, other_col)
        )

    def delta_copy(h):
        return remote(
            delta.at[h], partner_delta.at[h], pd_send.at[h], pd_recv.at[h], (other_seg, col)
        )

    def run_copy(h):
        peer = (lax.rem(pair + 1, n_pairs) * 2 + odd, col)
        return remote(running.at[h], arrived.at[h], run_send.at[h], run_recv.at[h], peer)

    def rows_copy(b):
        rows = pl.ds(*blocks[b])
        return remote(
            own_rows.at[rows], partner_rows.at[rows], rows_send.at[b], rows_recv.at[b],
            (seg, other_col),
        )

    def cross_copy(o, b):
        rows = pl.ds(*blocks[b])
        peer = (seg, lax.rem(chip + o, n_chips) * 2 + core)
        return remote(
            cross_out.at[o - 1, rows], cross_in.at[o - 1, rows],
            cross_send.at[o - 1, b], cross_recv.at[o - 1, b], peer,
        )

    def head_cols(h):
        return pl.ds(pl.multiple_of(h * HD, HD), HD)

    gate_values = 1.0 / (1.0 + jnp.exp(-gate_ref[...]))
    for h in range(heads):
        gates[0:1, h * HD : (h + 1) * HD] = jnp.broadcast_to(gate_values[0:1, h : h + 1], (1, HD))

    loads[0].wait()
    loads[1].wait()
    loads[2].start()
    for t in range(n_chips):
        w_copy(t).start()
        w_loads[t].start()

    @pl.loop(0, heads)
    def _(h):
        feat = features(k_ref[:, head_cols(h)].astype(F32))
        memory = tn_dot(v_ref[:, head_cols(h)], feat.astype(BF16))
        normal = jnp.sum(feat, axis=0, keepdims=True)
        delta[h, 0:HD, :] = memory.astype(BF16)
        delta[h, HD:MEM_ROWS, :] = jnp.broadcast_to(normal, (MEM_ROWS - HD, HD)).astype(BF16)
        delta_copy(h).start()

    loads[2].wait()

    scale = math.log2(math.e) / math.sqrt(HD)

    def attend(h):
        cols = head_cols(h)
        gate = 1.0 - gates[0:1, cols]
        ones = jnp.ones((tokens, HD), BF16)
        value_ext = jnp.concatenate([v_ref[:, cols], ones], axis=1)
        keys = k_ref[:, cols]
        row_ids = lax.broadcasted_iota(jnp.int32, (block, block), 0)
        col_ids = lax.broadcasted_iota(jnp.int32, (block, block), 1)
        allowed = col_ids <= row_ids
        for b in range(tokens // block):
            first = b * block
            query = q_ref[first : first + block, cols]
            diag = nt_dot(query, keys[first : first + block])
            diag = jnp.where(allowed, diag * scale, masked_score)
            top = jnp.max(diag, axis=1, keepdims=True)
            if b:
                past = nt_dot(query, keys[:first]) * scale
                top = jnp.maximum(top, jnp.max(past, axis=1, keepdims=True))
            total = jnp.dot(
                jnp.exp2(diag - top).astype(BF16), value_ext[first : first + block],
                preferred_element_type=F32,
            )
            if b:
                total = total + jnp.dot(
                    jnp.exp2(past - top).astype(BF16), value_ext[:first],
                    preferred_element_type=F32,
                )
            mixed[first : first + block, cols] = gate * (total[:, :HD] / total[:, HD:])

    odd_mask = jnp.where(odd == 1, 1.0, 0.0).astype(F32)

    def finish_head(b, h):
        rows = pl.ds(*blocks[b])
        cols = head_cols(h)
        feat = features(q_ref[rows, cols].astype(F32)).astype(BF16)
        both = nt_dot(feat, prior[h])
        retrieved = both[:, :HD] / jnp.maximum(both[:, HD:], 1.0)
        own_rows[rows, cols] = (gates[0:1, cols] * retrieved + mixed[rows, cols]).astype(BF16)

    def relay(h):
        delta_copy(h).wait_recv()
        theirs = partner_delta[h].astype(F32)

        @pl.when(pair == 0)
        def _():
            arrived[h] = jnp.zeros((MEM_ROWS, HD), BF16)

        @pl.when(pair > 0)
        def _():
            run_copy(h).wait_recv()

        before = arrived[h].astype(F32)

        @pl.when(pair + 1 < n_pairs)
        def _():
            running[h] = (before + (delta[h].astype(F32) + theirs)).astype(BF16)
            run_copy(h).start()

        mine = before + theirs * odd_mask
        prior[h, 0:HD, :] = mine[0:HD].astype(BF16)
        prior[h, HD : 2 * HD, :] = jnp.broadcast_to(mine[HD : HD + 1], (HD, HD)).astype(BF16)

    lag = jnp.minimum(1 + 2 * pair, heads)

    @pl.loop(0, 2 * heads)
    def _(i):
        @pl.when(i < heads)
        def _():
            attend(i)

        h = i - lag

        @pl.when((h >= 0) & (h < heads))
        def _():
            relay(h)

    for t in range(n_chips):
        w_loads[t].wait()
        w_copy(t).wait_recv()

    group = 2 if heads % 2 == 0 else 1

    def finish(b):
        @pl.loop(0, heads // group)
        def _(i):
            for g in range(group):
                finish_head(b, i * group + g)

        rows_copy(b).start()

    def product(b, target, t):
        rows = pl.ds(*blocks[b])
        cols = pl.ds(pl.multiple_of(t * tile, tile), tile)
        return jnp.dot(
            own_rows[rows], w_ref[0, target, :, cols], preferred_element_type=F32
        ) + jnp.dot(
            partner_rows[rows], w_ref[1, target, :, cols], preferred_element_type=F32
        )

    def cross(b):
        rows_copy(b).wait_recv()
        for o in range(1, n_chips):
            target = lax.rem(chip + o, n_chips)

            @pl.loop(0, width // tile)
            def _(t):
                cols = pl.ds(pl.multiple_of(t * tile, tile), tile)
                cross_out[o - 1, pl.ds(*blocks[b]), cols] = product(b, target, t).astype(BF16)

            cross_copy(o, b).start()

    finish(0)
    for b in range(n_blocks):
        if b + 1 < n_blocks:
            finish(b + 1)
        cross(b)

    for b in range(n_blocks):
        @pl.loop(0, width // tile)
        def _(t):
            cols = pl.ds(pl.multiple_of(t * tile, tile), tile)
            mixed[pl.ds(*blocks[b]), cols] = product(b, chip, t)

    for b in range(n_blocks):
        rows = pl.ds(*blocks[b])
        total = mixed[rows]
        for o in range(1, n_chips):
            cross_copy(o, b).wait_recv()
            total = total + cross_in[o - 1, rows].astype(F32)
        out_ref[rows] = total.astype(BF16)

    for t in range(n_chips):
        w_copy(t).wait_send()

    @pl.loop(0, heads)
    def _(h):
        delta_copy(h).wait_send()

        @pl.when(pair + 1 < n_pairs)
        def _():
            run_copy(h).wait_send()

    for b in range(n_blocks):
        rows_copy(b).wait_send()
        for o in range(1, n_chips):
            cross_copy(o, b).wait_send()


def local(n_ctx, n_heads, queries, keys, values, gate_bias, out_weight):
    tokens, width = queries.shape
    heads = gate_bias.shape[0]
    block = min(256, tokens)
    tile = min(512, width)
    sizes = [block] * (tokens // block)
    if len(sizes) > 1 and block % 32 == 0:
        sizes = [block // 2] + [block] * (len(sizes) - 1) + [block // 2]
    blocks = [(sum(sizes[:b]), size) for b, size in enumerate(sizes)]
    n_blocks = len(blocks)
    n_chips = n_heads // 2
    dma = pltpu.SemaphoreType.DMA
    far_chips = max(n_chips - 1, 1)
    hbm = pl.BlockSpec(memory_space=pltpu.HBM)
    memories = (heads, MEM_ROWS, HD)
    return pl.pallas_call(
        functools.partial(kernel, n_ctx, n_heads, block, blocks, tile),
        out_shape=jax.ShapeDtypeStruct((tokens, width), BF16),
        in_specs=[hbm, hbm, hbm, hbm, pl.BlockSpec(memory_space=pltpu.VMEM)],
        out_specs=pl.BlockSpec(memory_space=pltpu.VMEM),
        scratch_shapes=[
            pltpu.VMEM((tokens, width), BF16),
            pltpu.VMEM((tokens, width), BF16),
            pltpu.VMEM((tokens, width), BF16),
            pltpu.VMEM((2, n_chips, width, width), BF16),
            pltpu.VMEM((1, width), F32),
            pltpu.VMEM(memories, BF16),
            pltpu.VMEM(memories, BF16),
            pltpu.VMEM(memories, BF16),
            pltpu.VMEM(memories, BF16),
            pltpu.VMEM((heads, 2 * HD, HD), BF16),
            pltpu.VMEM((tokens, width), F32),
            pltpu.VMEM((tokens, width), BF16),
            pltpu.VMEM((tokens, width), BF16),
            pltpu.VMEM((far_chips, tokens, width), BF16),
            pltpu.VMEM((far_chips, tokens, width), BF16),
            dma((3,)),
            dma((n_chips,)),
            dma((n_chips,)),
            dma((n_chips,)),
            dma((heads,)),
            dma((heads,)),
            dma((heads,)),
            dma((heads,)),
            dma((n_blocks,)),
            dma((n_blocks,)),
            dma((far_chips, n_blocks)),
            dma((far_chips, n_blocks)),
        ],
        compiler_params=pltpu.CompilerParams(
            collective_id=0, has_side_effects=True, vmem_limit_bytes=63_000 * 1024
        ),
    )(queries, keys, values, out_weight, gate_bias.reshape(1, heads))


def solution(mesh):
    return jax.shard_map(
        functools.partial(local, mesh.shape["ctx"], mesh.shape["heads"]),
        mesh=mesh,
        in_specs=(
            P("ctx", "heads"),
            P("ctx", "heads"),
            P("ctx", "heads"),
            P("heads"),
            P("heads", None),
        ),
        out_specs=P("ctx", "heads"),
        check_vma=False,
    )
```

time: 92.1 us -> 85.5 us (0.928)
  Pallas kernels: 88.8 us -> 82.2 us
    pallas_call x1, Pallas kernels: 88.8 us -> 82.2 us  [local(): pl.pallas_call(functools.partial(kernel, n_ctx, n_heads, block, blocks, t...]
where the time goes in v2:
time: 85.5 us; the launch traced here: 85.3 us
  Pallas kernels  82.2 us (96%)
  local copies, waits for them, and re-layouts  3.08 us (4%)
    pallas_call x1, Pallas kernels, local(): pl.pallas_call(functools.partial(kernel, n_ctx, n_heads, block, blocks, t...  82.2 us
    unnamed x1, local copies, waits for them, and re-layouts  3.08 us

profile of v2, /device:TPU:29, one launch (start us, length us, event | category | flops | bytes accessed | tf_op | source)
XLA Modules:
  0.0 85.3 jit_solution(6478824840145368917)
XLA Ops:
  0.0 82.2 %shard_map.55 = bf16[1024,1024]{1,0:T(8,128)(2,1)} custom-call(bf16[1024,1024]{1,0:T(8,128)(2,1)} %q_hbm.1, bf16[1024,1024]{1,0:T(8,128)(2,1)} %k_hbm.1, bf16[1024,1024]{1,0:T(8,128)(2,1)} %v_hbm.1, bf16[1024,4096]{1,0:T(8,128)(2,1)} %w_hbm.1, f32[1,8]{1,0:T(1,128)} %bitcast.1), custom_call_target="tpu_custom_call" | custom-call | tf_op jit(solution)/shard_map/pallas_call | solution.py:303
  82.2 3.1 %copy.7 = bf16[1024,1024]{1,0:T(8,128)(2,1)} copy(bf16[1024,1024]{1,0:T(8,128)(2,1)} %shard_map.55) | data formatting | bytes 4194304
